TPU v7x, 32 devices: a whole 2x2x4 slice. The times are simulated.
32 devices in a mesh: rows: 8 (over z, y), cols: 4 (over x, core).
Axes of the slice: x: 2, y: 2, z: 4, core: 2. Of those that a mesh axis runs over, the one named last changes fastest.
Arguments:
- gradient: float32 [8192, 29568], P('rows', 'cols'), as said below
- start_block: float32 [29568, 64], P('cols'), may hold values from -0.03125 to 0.03125
- activations: float32 [512, 29568], P('rows', 'cols'), may hold values from -6 to 6
- out_grads: float32 [512, 8192], P('rows', 'cols'), may hold values from -6 to 6
Outputs:
- left_factor: float32 [8192, 64], P('rows')
- right_factor: float32 [29568, 64], P('cols')
- scores: float32 [512], P('rows')
Inputs may be any that keep to these rules, and one draw needn't show every extreme that they name: real-valued gradient entries, of order 29568 ** -0.5.
All inputs are finite; a program needn't handle non-finite values.
Results may differ from a plain program's by a relative error of at most 0.00013.
Values sent between devices are 32-bit elements; how exact they have to be, the bound alone decides.
A program may use at most 128 MiB of HBM per device.

v0:
```python
import jax
import jax.numpy as jnp
from jax import lax
from jax.sharding import PartitionSpec as P

ITERS = 2
HIGH = lax.Precision.HIGHEST


def factor_with(block, gram):
    lower = jnp.linalg.cholesky(gram)
    return (
        lax.linalg.triangular_solve(lower, block, left_side=False, lower=True, transpose_a=True),
        lower,
    )


def inner_gram(block):
    return jnp.dot(block.T, block, precision=HIGH, preferred_element_type=jnp.float32)


def per_device(gradient, start_block, activations, out_grads):
    grad_cols = out_grads.shape[1]
    col_index = lax.axis_index("cols")
    omega = start_block
    for step in range(ITERS):
        ysum = lax.psum(
            jnp.dot(gradient, omega, precision=HIGH, preferred_element_type=jnp.float32), "cols"
        )
        gram = lax.psum(inner_gram(ysum), "rows")
        left, lower_y = factor_with(ysum, gram)
        partial_z = jnp.dot(gradient.T, left, precision=HIGH, preferred_element_type=jnp.float32)
        zsum = lax.psum(partial_z, "rows")
        zgram = lax.psum(inner_gram(zsum), "cols")
        right, lower_z = factor_with(zsum, zgram)
        omega = right
    whole_rows = lax.all_gather(left, "rows", axis=0, tiled=True)
    left_cols = lax.dynamic_slice_in_dim(whole_rows, col_index * grad_cols, grad_cols, 0)
    left_part = jnp.dot(out_grads, left_cols, precision=HIGH, preferred_element_type=jnp.float32)
    right_part = jnp.dot(activations, right, precision=HIGH, preferred_element_type=jnp.float32)
    token_left, token_right = lax.psum((left_part, right_part), "cols")
    mixed = jnp.dot(token_left, lower_z, precision=HIGH, preferred_element_type=jnp.float32)
    scores = jnp.sum(mixed * token_right, axis=1)
    return (left, right, scores)


def solution(mesh):
    placed = (P("rows", "cols"), P("cols", None), P("rows", "cols"), P("rows", "cols"))
    return jax.shard_map(
        per_device,
        mesh=mesh,
        in_specs=placed,
        out_specs=(P("rows", None), P("cols", None), P("rows")),
        check_vma=False,
    )
```

profile of v0, /device:TPU:0, one launch (start us, length us, event | category | flops | bytes accessed | tf_op | source)
XLA Modules:
  0.0 579.3 jit_solution(6776016720726716855)
XLA Ops:
  7.2 1.5 copy-done
  8.7 24.2 %fusion.23 = f32[1024,64]{0,1:T(8,128)} fusion(f32[1024,7392]{0,1:T(8,128)} %param.9, f32[7392,64]{0,1:T(8,128)S(1)} %copy-done), kind=kOutput, calls=%fused_computation.50 | convolution fusion | flops 5813305344 | bytes 32432128 | tf_op jit(solution)/shard_map/dot_general | solution.py:28
  33.0 35.1 %all-reduce.6.cloned.1.call-done = f32[1024,64]{0,1:T(8,128)} async-done(((f32[1024,64]{0,1:T(8,128)}), f32[1024,64]{0,1:T(8,128)}) %all-reduce.6.cloned.1.call-update) | async-done | bytes 262160 | tf_op jit(solution)/shard_map/psum | solution.py:27
  68.1 1.4 fusion.24
  69.5 37.5 %psum.71 = f32[64,64]{0,1:T(8,128)S(1)} all-reduce(f32[64,64]{0,1:T(8,128)S(1)} %fusion.24), channel_id=1, replica_groups=mesh['rows'=8,'cols'=4] {'rows'}, use_global_device_ids=true, to_apply=%region_1.0 | all-reduce | flops 4096 | bytes 32768 | tf_op jit(solution)/shard_map/psum | solution.py:30
  107.1 5.8 %cholesky.74 = f32[64,64]{1,0:T(8,128)S(1)} custom-call(f32[64,64]{1,0:T(8,128)S(1)} %fusion.12), custom_call_target="Cholesky" | custom-call | tf_op jit(solution)/shard_map/jit(cholesky)/cholesky | solution.py:11
  114.3 4.9 custom-call.10
  120.6 30.9 %convolution_bitcast_fusion.3 = f32[7392,64]{0,1:T(8,128)} fusion(f32[1024,64]{0,1:T(8,128)S(1)} %convolution_bitcast_fusion.5, f32[1024,7392]{0,1:T(8,128)} %param.9), kind=kOutput, calls=%fused_computation.3 | convolution fusion | flops 5813305344 | bytes 32432128 | tf_op jit(solution)/shard_map/dot_general | solution.py:32
  151.5 93.6 %all-reduce.8.cloned.1.call-done = f32[7392,64]{0,1:T(8,128)} async-done(((f32[7392,64]{0,1:T(8,128)}), f32[7392,64]{0,1:T(8,128)}) %all-reduce.8.cloned.1.call-update) | async-done | bytes 1892368 | tf_op jit(solution)/shard_map/psum | solution.py:33
  245.1 3.8 fusion.25
  248.9 11.9 %psum.73 = f32[64,64]{0,1:T(8,128)S(1)} all-reduce(f32[64,64]{0,1:T(8,128)S(1)} %fusion.25), channel_id=1, replica_groups=mesh['rows'=8,'cols'=4] {'cols'}, use_global_device_ids=true, to_apply=%region_5.8 | all-reduce | flops 4096 | bytes 32768 | tf_op jit(solution)/shard_map/psum | solution.py:34
  260.9 5.8 %cholesky.85 = f32[64,64]{1,0:T(8,128)S(1)} custom-call(f32[64,64]{1,0:T(8,128)S(1)} %fusion.10), custom_call_target="Cholesky" | custom-call | tf_op jit(solution)/shard_map/jit(cholesky)/cholesky | solution.py:11
  268.1 4.9 custom-call.11
  273.0 3.3 convolution_bitcast_fusion.2
  276.2 23.1 %convolution_bitcast_fusion.6 = f32[1024,64]{0,1:T(8,128)} fusion(f32[7392,64]{0,1:T(8,128)S(1)} %convolution_bitcast_fusion.2, f32[1024,7392]{0,1:T(8,128)} %param.9), kind=kOutput, calls=%fused_computation.6 | convolution fusion | flops 5813305344 | bytes 32432128 | tf_op jit(solution)/shard_map/dot_general | solution.py:28
  299.4 31.0 %all-reduce.10.cloned.1.call-done = f32[1024,64]{0,1:T(8,128)} async-done(((f32[1024,64]{0,1:T(8,128)}), f32[1024,64]{0,1:T(8,128)}) %all-reduce.10.cloned.1.call-update) | async-done | bytes 262160 | tf_op jit(solution)/shard_map/psum | solution.py:27
  330.5 1.4 fusion.26
  331.9 37.4 %psum.75 = f32[64,64]{0,1:T(8,128)S(1)} all-reduce(f32[64,64]{0,1:T(8,128)S(1)} %fusion.26), channel_id=1, replica_groups=mesh['rows'=8,'cols'=4] {'rows'}, use_global_device_ids=true, to_apply=%region_7.11 | all-reduce | flops 4096 | bytes 32768 | tf_op jit(solution)/shard_map/psum | solution.py:30
  369.4 5.8 %cholesky.96 = f32[64,64]{1,0:T(8,128)S(1)} custom-call(f32[64,64]{1,0:T(8,128)S(1)} %fusion.8), custom_call_target="Cholesky" | custom-call | tf_op jit(solution)/shard_map/jit(cholesky)/cholesky | solution.py:11
  376.6 4.9 custom-call.12
  381.5 1.4 convolution_bitcast_fusion.4
  382.9 31.0 %convolution_bitcast_fusion.1 = f32[7392,64]{0,1:T(8,128)} fusion(f32[1024,64]{0,1:T(8,128)S(1)} %convolution_bitcast_fusion.4, f32[1024,7392]{0,1:T(8,128)} %param.9), kind=kOutput, calls=%fused_computation.1 | convolution fusion | flops 5813305344 | bytes 32432128 | tf_op jit(solution)/shard_map/dot_general | solution.py:32
  414.5 93.0 %all-reduce.12.cloned.1.call-done = f32[7392,64]{0,1:T(8,128)} async-done(((f32[7392,64]{0,1:T(8,128)}), f32[7392,64]{0,1:T(8,128)}) %all-reduce.12.cloned.1.call-update) | async-done | bytes 1892368 | tf_op jit(solution)/shard_map/psum | solution.py:33
  507.4 3.8 fusion.27
  511.2 11.6 %psum.77 = f32[64,64]{0,1:T(8,128)S(1)} all-reduce(f32[64,64]{0,1:T(8,128)S(1)} %fusion.27), channel_id=1, replica_groups=mesh['rows'=8,'cols'=4] {'cols'}, use_global_device_ids=true, to_apply=%region_9.13 | all-reduce | flops 4096 | bytes 32768 | tf_op jit(solution)/shard_map/psum | solution.py:34
  522.9 5.8 %cholesky.107 = f32[64,64]{1,0:T(8,128)S(1)} custom-call(f32[64,64]{1,0:T(8,128)S(1)} %fusion.6), custom_call_target="Cholesky" | custom-call | tf_op jit(solution)/shard_map/jit(cholesky)/cholesky | solution.py:11
  530.0 4.9 custom-call.13
  534.9 3.4 convolution_bitcast_fusion
  539.6 1.7 convolution_bitcast_fusion.7
  541.3 17.6 %all-gather.2.cloned.1.call-done = f32[8192,64]{0,1:T(8,128)} async-done(((f32[1024,64]{0,1:T(8,128)}), f32[8192,64]{0,1:T(8,128)}) %all-gather.2.cloned.1.call-update) | async-done | bytes 2097168 | tf_op jit(solution)/shard_map/all_gather | solution.py:37
  558.9 1.6 convolution_bitcast_fusion.8
  560.5 10.7 %all-reduce = (f32[64,64]{0,1:T(8,128)S(1)}, f32[64,64]{0,1:T(8,128)S(1)}) all-reduce(f32[64,64]{0,1:T(8,128)S(1)} %convolution_bitcast_fusion.7, f32[64,64]{0,1:T(8,128)S(1)} %convolution_bitcast_fusion.8), channel_id=1, replica_groups=mesh['rows'=8,'cols'=4] {'cols'}, use_global_device_ids=true, to_apply=%region_11.15 | all-reduce | flops 8192 | bytes 65536 | tf_op jit(solution)/shard_map/psum | solution.py:41
  (41 shorter events, 10.3 us)
Async XLA Ops:
  7.2 1.5 copy-start
  7.2 60.9 %all-reduce.6.cloned.1.call-start = ((), (), s32[]{:S(2)}) async-start(), calls=%async_computation | async-start | bytes 524288 | tf_op jit(solution)/shard_map/psum | solution.py:27
  32.9 212.2 %all-reduce.8.cloned.1.call-start = ((), (), s32[]{:S(2)}) async-start(), calls=%async_computation.1 | async-start | bytes 3801088 | tf_op jit(solution)/shard_map/psum | solution.py:33
  151.5 179.0 %all-reduce.10.cloned.1.call-start = ((), (), s32[]{:S(2)}) async-start(), calls=%async_computation.2 | async-start | bytes 524288 | tf_op jit(solution)/shard_map/psum | solution.py:27
  299.4 208.0 %all-reduce.12.cloned.1.call-start = ((), (), s32[]{:S(2)}) async-start(), calls=%async_computation.3 | async-start | bytes 3801088 | tf_op jit(solution)/shard_map/psum | solution.py:33
  382.8 31.0 %copy-start.2 = (f32[1024,64]{0,1:T(8,128)}, f32[1024,64]{0,1:T(8,128)S(1)}, u32[]{:S(2)}) copy-start(f32[1024,64]{0,1:T(8,128)S(1)} %convolution_bitcast_fusion.4) | copy-start | bytes 786436
  413.9 145.0 %all-gather.2.cloned.1.call-start = ((), (), s32[]{:S(2)}) async-start(), calls=%async_computation.4 | async-start | bytes 2359296 | tf_op jit(solution)/shard_map/all_gather | solution.py:37
  534.9 4.7 copy-start.3
  538.3 1.3 copy-start.1
  539.6 19.3 %copy-start.4 = (f32[64,2048]{1,0:T(8,128)S(1)}, f32[64,2048]{1,0:T(8,128)}, u32[]{:S(2)}) copy-start(f32[64,2048]{1,0:T(8,128)} %param.12) | copy-start | bytes 1572868
Sparse Core Ops, SparseCore 0:
  33.0 35.0 all-reduce.5
  151.6 93.4 all-reduce.7
  299.5 30.9 all-reduce.9
  414.0 93.4 all-reduce.11
  510.1 48.7 all-gather.1
where the time goes:
time: 583 us; the launch traced here: 579 us
  waiting for transfers between devices  271 us (46%)
  matrix products  133 us (23%)
  blocking collectives  109 us (19%)
  other arithmetic  48.2 us (8%)
  between operations  14.2 us (2%)
    psum x2, waiting for transfers between devices, per_device(): zsum = lax.psum(partial_z, 'rows')  187 us
    psum x2, blocking collectives, per_device(): gram = lax.psum(inner_gram(ysum), 'rows')  74.9 us
    psum x2, waiting for transfers between devices, per_device(): lax.psum(jnp.dot(gradient, omega, precision=HIGH, preferred_element_type=...  66.2 us
    dot_general x2, matrix products, per_device(): jnp.dot(gradient.T, left, precision=HIGH, preferred_element_type=jnp.floa...  61.9 us
    dot_general x2, matrix products, per_device(): jnp.dot(gradient, omega, precision=HIGH, preferred_element_type=jnp.float32)  47.3 us
    another operation x12, other arithmetic, factor_with(): lower = jnp.linalg.cholesky(gram)  26.1 us
    psum x2, blocking collectives, per_device(): zgram = lax.psum(inner_gram(zsum), 'cols')  23.5 us
    another operation x8, other arithmetic, factor_with(): lax.linalg.triangular_solve(lower, block, left_side=False, lower=True, tr...  22.1 us
  transfers between devices with their start and end apart: 5, of which 5 were waited for; matrix products, arithmetic and copies ran while one was open for 4% of the time, Pallas kernels for 0%

commit v1 on v0

--- a/solution.py
+++ b/solution.py
@@ -30,7 +30,9 @@
         gram = lax.psum(inner_gram(ysum), "rows")
         left, lower_y = factor_with(ysum, gram)
         partial_z = jnp.dot(gradient.T, left, precision=HIGH, preferred_element_type=jnp.float32)
-        zsum = lax.psum(partial_z, "rows")
+        zsum = partial_z
+        for hop in (1, 2, 4):
+            zsum = zsum + lax.ppermute(zsum, "rows", [(dev, dev ^ hop) for dev in range(8)])
         zgram = lax.psum(inner_gram(zsum), "cols")
         right, lower_z = factor_with(zsum, zgram)
         omega = right

time: 583 us -> 679 us (1.16)
  waiting for transfers between devices: 271 us -> 369 us
  matrix products: 133 us -> 126 us
    ppermute x0 -> x6, waiting for transfers between devices: none -> 303 us  [per_device(): lax.ppermute(zsum, 'rows', [(dev, dev ^ hop) for dev in range(8)])]
    psum x2 -> x0, waiting for transfers between devices: 187 us -> none  [per_device(): zsum = lax.psum(partial_z, 'rows')]
    all_gather x1, waiting for transfers between devices: 17.6 us -> 0.02 us  [per_device(): whole_rows = lax.all_gather(left, 'rows', axis=0, tiled=True)]
  transfers between devices with their start and end apart: 5 -> 9, of which waited for: 5 -> 8; matrix products, arithmetic and copies ran while one was open for 4% -> 1% of each run, Pallas kernels for 0% -> 0%
where the time goes in v1:
time: 679 us; the launch traced here: 675 us
  waiting for transfers between devices  369 us (54%)
  matrix products  126 us (19%)
  blocking collectives  109 us (16%)
  other arithmetic  53.3 us (8%)
  between operations  14.4 us (2%)
    ppermute x6, waiting for transfers between devices, per_device(): lax.ppermute(zsum, 'rows', [(dev, dev ^ hop) for dev in range(8)])  303 us
    psum x2, blocking collectives, per_device(): gram = lax.psum(inner_gram(ysum), 'rows')  74.9 us
    psum x2, waiting for transfers between devices, per_device(): lax.psum(jnp.dot(gradient, omega, precision=HIGH, preferred_element_type=...  65.8 us
    dot_general x2, matrix products, per_device(): jnp.dot(gradient.T, left, precision=HIGH, preferred_element_type=jnp.floa...  59.6 us
    dot_general x2, matrix products, per_device(): jnp.dot(gradient, omega, precision=HIGH, preferred_element_type=jnp.float32)  47.3 us
    another operation x12, other arithmetic, factor_with(): lower = jnp.linalg.cholesky(gram)  26.2 us
    another operation x8, other arithmetic, factor_with(): lax.linalg.triangular_solve(lower, block, left_side=False, lower=True, tr...  22.2 us
    psum x2, blocking collectives, per_device(): zgram = lax.psum(inner_gram(zsum), 'cols')  21.9 us
  transfers between devices with their start and end apart: 9, of which 8 were waited for; matrix products, arithmetic and copies ran while one was open for 1% of the time, Pallas kernels for 0%

profile of v1, /device:TPU:0, one launch (start us, length us, event | category | flops | bytes accessed | tf_op | source)
XLA Modules:
  0.0 675.3 jit_solution(4455810772178750433)
XLA Ops:
  8.7 24.2 %fusion.23 = f32[1024,64]{0,1:T(8,128)} fusion(f32[1024,7392]{0,1:T(8,128)} %param.9, f32[7392,64]{0,1:T(8,128)S(1)} %copy-done), kind=kOutput, calls=%fused_computation.50 | convolution fusion | flops 5813305344 | bytes 32432128 | tf_op jit(solution)/shard_map/dot_general | solution.py:28
  33.0 35.1 %all-reduce.4.cloned.1.call-done = f32[1024,64]{0,1:T(8,128)} async-done(((f32[1024,64]{0,1:T(8,128)}), f32[1024,64]{0,1:T(8,128)}) %all-reduce.4.cloned.1.call-update) | async-done | bytes 262160 | tf_op jit(solution)/shard_map/psum | solution.py:27
  69.5 37.5 %psum.57 = f32[64,64]{0,1:T(8,128)S(1)} all-reduce(f32[64,64]{0,1:T(8,128)S(1)} %fusion.24), channel_id=1, replica_groups=mesh['rows'=8,'cols'=4] {'rows'}, use_global_device_ids=true, to_apply=%region_1.0 | all-reduce | flops 4096 | bytes 32768 | tf_op jit(solution)/shard_map/psum | solution.py:30
  107.1 5.8 cholesky.74
  114.2 4.9 custom-call.10
  120.5 29.8 %convolution_bitcast_fusion.3 = f32[7392,64]{0,1:T(8,128)S(1)} fusion(f32[1024,64]{0,1:T(8,128)S(1)} %convolution_bitcast_fusion.5, f32[1024,7392]{0,1:T(8,128)} %param.9), kind=kOutput, calls=%fused_computation.3 | convolution fusion | flops 5813305344 | bytes 32432128 | tf_op jit(solution)/shard_map/dot_general | solution.py:32
  150.4 34.7 %collective-permute-done = f32[7392,64]{0,1:T(8,128)S(1)} collective-permute-done((f32[7392,64]{0,1:T(8,128)S(1)}, f32[7392,64]{0,1:T(8,128)S(1)}, u32[]{:S(2)}, u32[]{:S(2)}) %collective-permute-start) | collective-permute-done | bytes 1892384 | tf_op jit(solution)/shard_map/ppermute | solution.py:35
  185.4 38.9 %collective-permute-done.1 = f32[7392,64]{0,1:T(8,128)S(1)} collective-permute-done((f32[7392,64]{0,1:T(8,128)S(1)}, f32[7392,64]{0,1:T(8,128)S(1)}, u32[]{:S(2)}, u32[]{:S(2)}) %collective-permute-start.1) | collective-permute-done | bytes 1892384 | tf_op jit(solution)/shard_map/ppermute | solution.py:35
  224.8 69.6 %collective-permute-done.2 = f32[7392,64]{0,1:T(8,128)S(1)} collective-permute-done((f32[7392,64]{0,1:T(8,128)S(1)}, f32[7392,64]{0,1:T(8,128)S(1)}, u32[]{:S(2)}, u32[]{:S(2)}) %collective-permute-start.2) | collective-permute-done | bytes 1892384 | tf_op jit(solution)/shard_map/ppermute | solution.py:35
  296.3 11.4 %psum.58 = f32[64,64]{0,1:T(8,128)S(1)} all-reduce(f32[64,64]{0,1:T(8,128)S(1)} %fusion.25), channel_id=1, replica_groups=mesh['rows'=8,'cols'=4] {'cols'}, use_global_device_ids=true, to_apply=%region_4.7 | all-reduce | flops 4096 | bytes 32768 | tf_op jit(solution)/shard_map/psum | solution.py:36
  307.8 5.8 cholesky.85
  315.0 4.9 custom-call.11
  319.9 1.8 convolution_bitcast_fusion.2
  321.7 23.1 %convolution_bitcast_fusion.6 = f32[1024,64]{0,1:T(8,128)} fusion(f32[7392,64]{0,1:T(8,128)S(1)} %convolution_bitcast_fusion.2, f32[1024,7392]{0,1:T(8,128)} %param.9), kind=kOutput, calls=%fused_computation.6 | convolution fusion | flops 5813305344 | bytes 32432128 | tf_op jit(solution)/shard_map/dot_general | solution.py:28
  344.9 30.7 %all-reduce.6.cloned.1.call-done = f32[1024,64]{0,1:T(8,128)} async-done(((f32[1024,64]{0,1:T(8,128)}), f32[1024,64]{0,1:T(8,128)}) %all-reduce.6.cloned.1.call-update) | async-done | bytes 262160 | tf_op jit(solution)/shard_map/psum | solution.py:27
  376.9 37.4 %psum.60 = f32[64,64]{0,1:T(8,128)S(1)} all-reduce(f32[64,64]{0,1:T(8,128)S(1)} %fusion.26), channel_id=1, replica_groups=mesh['rows'=8,'cols'=4] {'rows'}, use_global_device_ids=true, to_apply=%region_6.10 | all-reduce | flops 4096 | bytes 32768 | tf_op jit(solution)/shard_map/psum | solution.py:30
  414.4 5.8 cholesky.96
  421.6 4.9 custom-call.12
  427.9 29.7 %convolution_bitcast_fusion.1 = f32[7392,64]{0,1:T(8,128)S(1)} fusion(f32[1024,64]{0,1:T(8,128)S(1)} %convolution_bitcast_fusion.4, f32[1024,7392]{0,1:T(8,128)} %param.9), kind=kOutput, calls=%fused_computation.1 | convolution fusion | flops 5813305344 | bytes 32432128 | tf_op jit(solution)/shard_map/dot_general | solution.py:32
  457.7 48.9 %collective-permute-done.3 = f32[7392,64]{0,1:T(8,128)} collective-permute-done((f32[7392,64]{0,1:T(8,128)S(1)}, f32[7392,64]{0,1:T(8,128)}, u32[]{:S(2)}, u32[]{:S(2)}) %collective-permute-start.3) | collective-permute-done | bytes 1892384 | tf_op jit(solution)/shard_map/ppermute | solution.py:35
  506.6 1.7 add.49
  508.4 41.3 %collective-permute-done.4 = f32[7392,64]{0,1:T(8,128)S(1)} collective-permute-done((f32[7392,64]{0,1:T(8,128)S(1)}, f32[7392,64]{0,1:T(8,128)S(1)}, u32[]{:S(2)}, u32[]{:S(2)}) %collective-permute-start.4) | collective-permute-done | bytes 1892384 | tf_op jit(solution)/shard_map/ppermute | solution.py:35
  550.1 2.0 convolution_bitcast_fusion.8
  552.1 69.4 %collective-permute-done.5 = f32[7392,64]{0,1:T(8,128)} collective-permute-done((f32[7392,64]{0,1:T(8,128)S(1)}, f32[7392,64]{0,1:T(8,128)}, u32[]{:S(2)}, u32[]{:S(2)}) %collective-permute-start.5) | collective-permute-done | bytes 1892384 | tf_op jit(solution)/shard_map/ppermute | solution.py:35
  621.5 2.3 add.51
  623.8 1.6 fusion.27
  625.5 10.5 %psum.61 = f32[64,64]{0,1:T(8,128)S(1)} all-reduce(f32[64,64]{0,1:T(8,128)S(1)} %fusion.27), channel_id=1, replica_groups=mesh['rows'=8,'cols'=4] {'cols'}, use_global_device_ids=true, to_apply=%region_7.11 | all-reduce | flops 4096 | bytes 32768 | tf_op jit(solution)/shard_map/psum | solution.py:36
  636.0 5.8 cholesky.107
  643.3 4.9 custom-call.13
  648.3 3.4 convolution_bitcast_fusion
  652.9 1.7 convolution_bitcast_fusion.7
  654.6 12.5 %all-reduce = (f32[64,64]{0,1:T(8,128)S(1)}, f32[64,64]{0,1:T(8,128)S(1)}) all-reduce(f32[64,64]{0,1:T(8,128)S(1)} %convolution_bitcast_fusion.7, f32[64,64]{0,1:T(8,128)S(1)} %convolution_bitcast_fusion.8), channel_id=1, replica_groups=mesh['rows'=8,'cols'=4] {'cols'}, use_global_device_ids=true, to_apply=%region_9.13 | all-reduce | flops 8192 | bytes 65536 | tf_op jit(solution)/shard_map/psum | solution.py:43
  (59 shorter events, 18.7 us)
Async XLA Ops:
  7.2 1.5 copy-start
  7.2 60.9 %all-reduce.4.cloned.1.call-start = ((), (), s32[]{:S(2)}) async-start(), calls=%async_computation | async-start | bytes 524288 | tf_op jit(solution)/shard_map/psum | solution.py:27
  32.9 342.6 %all-reduce.6.cloned.1.call-start = ((), (), s32[]{:S(2)}) async-start(), calls=%async_computation.1 | async-start | bytes 524288 | tf_op jit(solution)/shard_map/psum | solution.py:27
  150.4 34.8 %collective-permute-start = (f32[7392,64]{0,1:T(8,128)S(1)}, f32[7392,64]{0,1:T(8,128)S(1)}, u32[]{:S(2)}, u32[]{:S(2)}) collective-permute-start(f32[7392,64]{0,1:T(8,128)S(1)} %convolution_bitcast_fusion.3), channel_id=1, source_target_pairs={{0,4},{4,0},{8,12},{12,8},{16,20},{20,16},{24,28},{28,24},{1,5},{5... | collective-permute-start | bytes 5677064 | tf_op jit(solution)/shard_map/ppermute | solution.py:35
  185.4 39.0 %collective-permute-start.1 = (f32[7392,64]{0,1:T(8,128)S(1)}, f32[7392,64]{0,1:T(8,128)S(1)}, u32[]{:S(2)}, u32[]{:S(2)}) collective-permute-start(f32[7392,64]{0,1:T(8,128)S(1)} %add.46), channel_id=1, source_target_pairs={{0,8},{4,12},{8,0},{12,4},{16,24},{20,28},{24,16},{28,20},{1,9},{5... | collective-permute-start | bytes 5677064 | tf_op jit(solution)/shard_map/ppermute | solution.py:35
  224.8 69.7 %collective-permute-start.2 = (f32[7392,64]{0,1:T(8,128)S(1)}, f32[7392,64]{0,1:T(8,128)S(1)}, u32[]{:S(2)}, u32[]{:S(2)}) collective-permute-start(f32[7392,64]{0,1:T(8,128)S(1)} %add.47), channel_id=1, source_target_pairs={{0,16},{4,20},{8,24},{12,28},{16,0},{20,4},{24,8},{28,12},{1,17},{... | collective-permute-start | bytes 5677064 | tf_op jit(solution)/shard_map/ppermute | solution.py:35
  344.8 205.3 %all-gather.2.cloned.1.call-start = ((), (), s32[]{:S(2)}) async-start(), calls=%async_computation.2 | async-start | bytes 2359296 | tf_op jit(solution)/shard_map/all_gather | solution.py:39
  427.9 29.8 %copy-start.5 = (f32[1024,64]{0,1:T(8,128)}, f32[1024,64]{0,1:T(8,128)S(1)}, u32[]{:S(2)}) copy-start(f32[1024,64]{0,1:T(8,128)S(1)} %convolution_bitcast_fusion.4) | copy-start | bytes 786436
  457.6 49.0 %collective-permute-start.3 = (f32[7392,64]{0,1:T(8,128)S(1)}, f32[7392,64]{0,1:T(8,128)}, u32[]{:S(2)}, u32[]{:S(2)}) collective-permute-start(f32[7392,64]{0,1:T(8,128)S(1)} %convolution_bitcast_fusion.1), channel_id=1, source_target_pairs={{0,4},{4,0},{8,12},{12,8},{16,20},{20,16},{24,28},{28,24},{1,5},{5... | collective-permute-start | bytes 5677064 | tf_op jit(solution)/shard_map/ppermute | solution.py:35
  508.3 41.8 %copy-start.7 = (f32[64,2048]{1,0:T(8,128)S(1)}, f32[64,2048]{1,0:T(8,128)}, u32[]{:S(2)}) copy-start(f32[64,2048]{1,0:T(8,128)} %param.12) | copy-start | bytes 1572868
  508.3 41.4 %collective-permute-start.4 = (f32[7392,64]{0,1:T(8,128)S(1)}, f32[7392,64]{0,1:T(8,128)S(1)}, u32[]{:S(2)}, u32[]{:S(2)}) collective-permute-start(f32[7392,64]{0,1:T(8,128)S(1)} %add.49), channel_id=1, source_target_pairs={{0,8},{4,12},{8,0},{12,4},{16,24},{20,28},{24,16},{28,20},{1,9},{5... | collective-permute-start | bytes 5677064 | tf_op jit(solution)/shard_map/ppermute | solution.py:35
  550.0 2.1 copy-start.3
  550.0 71.5 %collective-permute-start.5 = (f32[7392,64]{0,1:T(8,128)S(1)}, f32[7392,64]{0,1:T(8,128)}, u32[]{:S(2)}, u32[]{:S(2)}) collective-permute-start(f32[7392,64]{0,1:T(8,128)S(1)} %add.50), channel_id=1, source_target_pairs={{0,16},{4,20},{8,24},{12,28},{16,0},{20,4},{24,8},{28,12},{1,17},{... | collective-permute-start | bytes 5677064 | tf_op jit(solution)/shard_map/ppermute | solution.py:35
  623.8 1.6 copy-start.2
  648.2 4.7 copy-start.6
  648.3 20.3 %copy-start.1 = (f32[7392,64]{0,1:T(8,128)S(1)}, f32[7392,64]{0,1:T(8,128)}, u32[]{:S(2)}) copy-start(f32[7392,64]{0,1:T(8,128)} %param.10) | copy-start | bytes 5677060
  651.7 1.3 copy-start.4
Sparse Core Ops, SparseCore 0:
  33.0 34.9 all-reduce.3
  344.9 30.5 all-reduce.5
  457.9 56.8 all-gather.1
